TPU v7x, 32 devices: a whole 2x2x4 slice. The times are simulated.
32 devices in a mesh: member: 2 (over core), section: 4 (over y, x), atoms: 4 (over z).
Axes of the slice: x: 2, y: 2, z: 4, core: 2. Of those that a mesh axis runs over, the one named last changes fastest.
Arguments:
- positions: float32 [8, 3, 512], P(None, None, 'atoms'), may hold values from -8 to 8
- atom_types: int32 [8, 512], P(None, 'atoms'), may hold values from 0 to 127
- neighbors: int32 [8, 512, 128], P(None, 'atoms'), may hold values from 0 to 511
- nbr_mask: int32 [8, 512, 128], P(None, 'atoms'), may hold values 0 or 1
- type_table: bfloat16 [2, 128, 128], P('member'), may hold values from -6 to 6
- norm_gain: bfloat16 [2, 4, 128], P('member', 'section'), may hold values from 0.25 to 1.75
- proj_weight: bfloat16 [2, 4, 128, 384], P('member', 'section'), may hold values from -0.5 to 0.5
- out_weight: bfloat16 [2, 4, 128, 128], P('member', 'section'), may hold values from -0.5 to 0.5
- force_coef: bfloat16 [2, 4, 4], P('member', 'section'), may hold values from -48 to 48
Outputs:
- atom_dev: float32 [8, 512], P('section', 'atoms')
- max_dev: float32 [8], P('section')
- mean_force: float32 [8, 3, 512], P('section', None, 'atoms')
Inputs may be any that keep to these rules, and one draw needn't show every extreme that they name: `neighbors`: indices of atoms of the same frame, repeats and the atom itself allowed.
All inputs are finite; a program needn't handle non-finite values. No bound on the sum of `nbr_mask` on one device may be relied on, other than what follows from the above.
Results may differ from a plain program's by a relative error of at most 0.013.
Values may be sent and summed in bfloat16 or wider, within the bound.
No kernel may reach another device: no remote copies, remote signals or barrier semaphores. Data moves between devices by JAX's collectives and lax.ppermute only.
A program may use at most 64 MiB of HBM per device.

v0:
```python
import math

import jax
import jax.numpy as jnp
from jax import lax
from jax.sharding import PartitionSpec as P


def geometry(nbr, mask, pos_all, pos_own):
    total_atoms = pos_all.shape[1]
    hit = (nbr[:, :, None] == lax.iota(jnp.int32, total_atoms)[None, None, :]).astype(jnp.float32)
    counts = jnp.sum(hit * mask.astype(jnp.float32)[:, :, None], 1)
    delta = pos_all[:, None, :] - pos_own[:, :, None]
    switch = 1.0 / (1.0 + 0.125 * jnp.sum(delta * delta, 0))
    return (counts * switch, delta)


def block_dev(h_in, gain, proj, outw, coef, pair, delta, slots):
    width = h_in.shape[1]
    heads = coef.shape[0]
    head_dim = width // heads
    count = h_in.shape[0]
    hf = h_in.astype(jnp.float32)
    normed = (
        hf * lax.rsqrt(jnp.mean(hf * hf, -1, keepdims=True) + 1e-06) * gain.astype(jnp.float32)
    ).astype(jnp.bfloat16)
    query = jnp.dot(normed, proj[:, :width], preferred_element_type=jnp.float32).astype(
        jnp.bfloat16
    )
    keyval = jnp.dot(
        lax.all_gather(normed, "atoms", axis=0, tiled=True),
        proj[:, width:],
        preferred_element_type=jnp.float32,
    ).astype(jnp.bfloat16)
    total_atoms = keyval.shape[0]
    query3 = query.reshape(count, heads, head_dim)
    keys = keyval[:, :width].reshape(total_atoms, heads, head_dim)
    values = keyval[:, width:].reshape(total_atoms, heads, head_dim)
    scores = jnp.einsum(
        "ahd,jhd->haj", query3, keys, preferred_element_type=jnp.float32
    ) / math.sqrt(head_dim)
    weights = jax.nn.sigmoid(scores) * pair[None]
    message = jnp.einsum(
        "haj,jhd->ahd", weights.astype(jnp.bfloat16), values, preferred_element_type=jnp.float32
    )
    message = (message / slots).reshape(count, width).astype(jnp.bfloat16)
    h_out = (hf + jnp.dot(message, outw, preferred_element_type=jnp.float32)).astype(jnp.bfloat16)
    pair_coef = jnp.einsum("h,haj->aj", coef.astype(jnp.float32), weights)
    force = jnp.einsum("aj,caj->ca", pair_coef, delta) / slots
    return (h_out, force)


def embed(types_now, table):
    onehot = (types_now[:, None] == lax.iota(jnp.int32, table.shape[0])[None, :]).astype(
        jnp.bfloat16
    )
    return jnp.dot(onehot, table, preferred_element_type=jnp.float32).astype(jnp.bfloat16)


def shards(
    positions,
    atom_types,
    neighbors,
    nbr_mask,
    type_table,
    norm_gain,
    proj_weight,
    out_weight,
    force_coef,
):
    n_section = lax.axis_size("section")
    section_idx = lax.axis_index("section")
    frames = atom_types.shape[0]
    per_section = frames // n_section
    count = atom_types.shape[1]
    slots = neighbors.shape[2]
    table = type_table[0]
    pos_all = lax.all_gather(positions, "atoms", axis=2, tiled=True)
    gains, projs, outs, coefs = (
        lax.all_gather(norm_gain, "section", axis=1, tiled=True),
        lax.all_gather(proj_weight, "section", axis=1, tiled=True),
        lax.all_gather(out_weight, "section", axis=1, tiled=True),
        lax.all_gather(force_coef, "section", axis=1, tiled=True),
    )
    first = section_idx * per_section

    def whole_frame(local, own_forces):
        frame = first + local
        nbr = lax.dynamic_index_in_dim(neighbors, frame, 0, keepdims=False)
        mask = lax.dynamic_index_in_dim(nbr_mask, frame, 0, keepdims=False)
        pos_now = lax.dynamic_index_in_dim(pos_all, frame, 0, keepdims=False)
        pos_own = lax.dynamic_index_in_dim(positions, frame, 0, keepdims=False)
        pair, delta = geometry(nbr, mask, pos_now, pos_own)
        h_cur = embed(lax.dynamic_index_in_dim(atom_types, frame, 0, keepdims=False), table)
        total = jnp.zeros((3, count), jnp.float32)
        for blk in range(n_section):
            h_cur, term = block_dev(
                h_cur, gains[0, blk], projs[0, blk], outs[0, blk], coefs[0, blk], pair, delta, slots
            )
            total = total + term
        return lax.dynamic_update_index_in_dim(own_forces, total, local, 0)

    own = lax.fori_loop(
        0, per_section, whole_frame, jnp.zeros((per_section, 3, count), jnp.float32)
    )
    members = lax.axis_size("member")
    mean_force = lax.psum(own, "member") / members
    centered = own - mean_force
    spread = lax.psum(jnp.sum(centered * centered, 1), "member") / members
    atom_dev = jnp.sqrt(spread)
    max_dev = lax.pmax(jnp.max(atom_dev, -1), "atoms")
    return (atom_dev, max_dev, mean_force)


def solution(mesh):
    return jax.shard_map(
        shards,
        mesh=mesh,
        in_specs=(
            P(None, None, "atoms"),
            P(None, "atoms"),
            P(None, "atoms", None),
            P(None, "atoms", None),
            P("member", None, None),
            P("member", "section", None),
            P("member", "section", None, None),
            P("member", "section", None, None),
            P("member", "section", None),
        ),
        out_specs=(P("section", "atoms"), P("section"), P("section", None, "atoms")),
        check_vma=False,
    )
```

profile of v0, /device:TPU:0, one launch (start us, length us, event | category | flops | bytes accessed | tf_op | source)
XLA Modules:
  0.0 200.3 jit_solution(8612434693529792498)
XLA Ops:
  0.6 9.5 %all_gather.44 = bf16[1,4,128]{2,0,1:T(2,128)(2,1)S(1)} all-gather(bf16[1,1,128]{2,0,1:T(2,128)(2,1)} %bitcast.301), channel_id=1, replica_groups=mesh['member'=2,'section'=4,'atoms'=4] {'section'}, dimensions={1}, use_global_device_ids=true | all-gather | bytes 1280 | tf_op jit(solution)/shard_map/all_gather | solution.py:80
  10.2 7.8 %all_gather.46 = bf16[1,4,4]{2,0,1:T(2,128)(2,1)S(1)} all-gather(bf16[1,1,4]{2,0,1:T(2,128)(2,1)} %bitcast.302), channel_id=1, replica_groups=mesh['member'=2,'section'=4,'atoms'=4] {'section'}, dimensions={1}, use_global_device_ids=true | all-gather | bytes 40 | tf_op jit(solution)/shard_map/all_gather | solution.py:83
  18.0 0.7 copy.31
  18.7 12.2 %all_gather.43 = f32[8,3,512]{2,1,0:T(4,128)S(1)} all-gather(f32[8,3,128]{2,1,0:T(4,128)S(1)} %copy.31), channel_id=1, replica_groups=mesh['member'=2,'section'=4,'atoms'=4] {'atoms'}, dimensions={2}, use_global_device_ids=true | all-gather | bytes 61440 | tf_op jit(solution)/shard_map/all_gather | solution.py:78
  30.9 7.7 %all_gather.47 = bf16[1,4,128,128]{3,2,0,1:T(8,128)(2,1)S(1)} all-gather(bf16[1,1,128,128]{3,2,0,1:T(8,128)(2,1)} %bitcast.300), channel_id=1, replica_groups=mesh['member'=2,'section'=4,'atoms'=4] {'section'}, dimensions={1}, use_global_device_ids=true | all-gather | bytes 163840 | tf_op jit(solution)/shard_map/all_gather | solution.py:82
  38.6 9.3 %all_gather.45 = bf16[1,4,128,384]{3,2,0,1:T(8,128)(2,1)S(1)} all-gather(bf16[1,1,128,384]{3,2,0,1:T(8,128)(2,1)} %bitcast.299), channel_id=1, replica_groups=mesh['member'=2,'section'=4,'atoms'=4] {'section'}, dimensions={1}, use_global_device_ids=true | all-gather | bytes 491520 | tf_op jit(solution)/shard_map/all_gather | solution.py:81
  47.9 137.4 %while.13 = (s32[]{:T(128)}, f32[2,3,128]{2,0,1:T(2,128)S(1)}, s32[]{:T(128)}, f32[8,3,512]{2,1,0:T(4,128)S(1)}, f32[8,3,128]{2,1,0:T(4,128)S(1)}, /*index=5*/s3...) while((s32[]{:T(128)}, f32[2,3,128]{2,0,1:T(2,128)S(1)}, ...), condition=%wide.region_7.8_spmd, body=%wide.region_0.7_spmd.sunk | while | flops 322554368 | bytes 20396256 | solution.py:103
  47.9 0.7 fusion.231
  49.0 0.9 convert_bitcast_fusion.2
  49.9 6.0 %select_reduce_fusion.2 = f32[128,512]{1,0:T(8,128)S(1)} fusion(f32[128,128]{1,0:T(8,128)S(1)} %get-tuple-element.420, s32[128,128]{1,0:T(8,128)S(1)} %get-tuple-element.421), kind=kLoop, calls=%fused_computation.clone.1 | loop fusion | flops 25100288 | bytes 393216 | tf_op jit(solution)/shard_map/while/body/eval_jaxpr/reduce_sum | solution.py:12
  55.8 12.3 %all_gather.52 = bf16[512,128]{0,1:T(8,128)(2,1)S(1)} all-gather(bf16[128,128]{0,1:T(8,128)(2,1)S(1)} %multiply_convert_fusion.8), channel_id=1, replica_groups=mesh['member'=2,'section'=4,'atoms'=4] {'atoms'}, dimensions={0}, use_global_device_ids=true | all-gather | bytes 163840 | tf_op jit(solution)/shard_map/while/body/eval_jaxpr/all_gather | solution.py:31
  68.7 0.3 convolution_convert_fusion.15
  69.0 0.5 fusion.233
  69.5 0.3 fusion.234
  69.7 0.5 fusion.249
  70.3 0.6 fusion.250
  71.6 12.3 %all_gather.53 = bf16[512,128]{0,1:T(8,128)(2,1)S(1)} all-gather(bf16[128,128]{0,1:T(8,128)(2,1)S(1)} %multiply_convert_fusion.9), channel_id=1, replica_groups=mesh['member'=2,'section'=4,'atoms'=4] {'atoms'}, dimensions={0}, use_global_device_ids=true | all-gather | bytes 163840 | tf_op jit(solution)/shard_map/while/body/eval_jaxpr/all_gather | solution.py:31
  83.8 0.3 convolution_convert_fusion.17
  84.1 0.5 fusion.236
  84.6 0.3 fusion.237
  84.9 0.5 fusion.247
  85.5 0.6 fusion.248
  86.8 12.3 %all_gather.54 = bf16[512,128]{0,1:T(8,128)(2,1)S(1)} all-gather(bf16[128,128]{0,1:T(8,128)(2,1)S(1)} %multiply_convert_fusion.10), channel_id=1, replica_groups=mesh['member'=2,'section'=4,'atoms'=4] {'atoms'}, dimensions={0}, use_global_device_ids=true | all-gather | bytes 163840 | tf_op jit(solution)/shard_map/while/body/eval_jaxpr/all_gather | solution.py:31
  99.0 0.3 convolution_convert_fusion.19
  99.3 0.5 fusion.239
  99.8 0.3 fusion.240
  100.1 0.5 fusion.245
  100.6 0.6 fusion.246
  101.9 12.5 %all_gather.55 = bf16[512,128]{0,1:T(8,128)(2,1)S(1)} all-gather(bf16[128,128]{0,1:T(8,128)(2,1)S(1)} %multiply_convert_fusion.11), channel_id=1, replica_groups=mesh['member'=2,'section'=4,'atoms'=4] {'atoms'}, dimensions={0}, use_global_device_ids=true | all-gather | bytes 163840 | tf_op jit(solution)/shard_map/while/body/eval_jaxpr/all_gather | solution.py:31
  114.4 0.3 fusion.241
  114.7 0.5 fusion.242
  115.2 0.5 fusion.243
  115.7 0.6 fusion.244
  116.5 0.7 fusion.231
  117.6 0.9 convert_bitcast_fusion.2
  118.5 6.0 %select_reduce_fusion.2 = f32[128,512]{1,0:T(8,128)S(1)} fusion(f32[128,128]{1,0:T(8,128)S(1)} %get-tuple-element.420, s32[128,128]{1,0:T(8,128)S(1)} %get-tuple-element.421), kind=kLoop, calls=%fused_computation.clone.1 | loop fusion | flops 25100288 | bytes 393216 | tf_op jit(solution)/shard_map/while/body/eval_jaxpr/reduce_sum | solution.py:12
  124.5 12.5 %all_gather.52 = bf16[512,128]{0,1:T(8,128)(2,1)S(1)} all-gather(bf16[128,128]{0,1:T(8,128)(2,1)S(1)} %multiply_convert_fusion.8), channel_id=1, replica_groups=mesh['member'=2,'section'=4,'atoms'=4] {'atoms'}, dimensions={0}, use_global_device_ids=true | all-gather | bytes 163840 | tf_op jit(solution)/shard_map/while/body/eval_jaxpr/all_gather | solution.py:31
  137.6 0.3 convolution_convert_fusion.15
  137.9 0.5 fusion.233
  138.4 0.3 fusion.234
  138.7 0.5 fusion.249
  139.2 0.6 fusion.250
  140.5 12.4 %all_gather.53 = bf16[512,128]{0,1:T(8,128)(2,1)S(1)} all-gather(bf16[128,128]{0,1:T(8,128)(2,1)S(1)} %multiply_convert_fusion.9), channel_id=1, replica_groups=mesh['member'=2,'section'=4,'atoms'=4] {'atoms'}, dimensions={0}, use_global_device_ids=true | all-gather | bytes 163840 | tf_op jit(solution)/shard_map/while/body/eval_jaxpr/all_gather | solution.py:31
  152.9 0.3 convolution_convert_fusion.17
  153.2 0.5 fusion.236
  153.6 0.3 fusion.237
  153.9 0.5 fusion.247
  154.5 0.6 fusion.248
  155.8 12.3 %all_gather.54 = bf16[512,128]{0,1:T(8,128)(2,1)S(1)} all-gather(bf16[128,128]{0,1:T(8,128)(2,1)S(1)} %multiply_convert_fusion.10), channel_id=1, replica_groups=mesh['member'=2,'section'=4,'atoms'=4] {'atoms'}, dimensions={0}, use_global_device_ids=true | all-gather | bytes 163840 | tf_op jit(solution)/shard_map/while/body/eval_jaxpr/all_gather | solution.py:31
  168.0 0.3 convolution_convert_fusion.19
  168.3 0.5 fusion.239
  168.8 0.3 fusion.240
  169.1 0.5 fusion.245
  169.6 0.6 fusion.246
  170.9 12.3 %all_gather.55 = bf16[512,128]{0,1:T(8,128)(2,1)S(1)} all-gather(bf16[128,128]{0,1:T(8,128)(2,1)S(1)} %multiply_convert_fusion.11), channel_id=1, replica_groups=mesh['member'=2,'section'=4,'atoms'=4] {'atoms'}, dimensions={0}, use_global_device_ids=true | all-gather | bytes 163840 | tf_op jit(solution)/shard_map/while/body/eval_jaxpr/all_gather | solution.py:31
  183.2 0.3 fusion.241
  183.5 0.5 fusion.242
  184.0 0.5 fusion.243
  184.5 0.6 fusion.244
  185.3 2.5 %psum.14 = f32[2,3,128]{2,0,1:T(2,128)S(1)} all-reduce(f32[2,3,128]{2,0,1:T(2,128)S(1)} %get-tuple-element.217), channel_id=1, replica_groups=mesh['member'=2,'section'=4,'atoms'=4] {'member'}, use_global_device_ids=true, to_apply=%region_8.9 | all-reduce | flops 768 | bytes 6144 | tf_op jit(solution)/shard_map/psum | solution.py:107
  187.8 0.6 multiply_reduce_fusion.5
  188.3 2.4 %psum.15 = f32[2,128]{1,0:T(2,128)S(1)} all-reduce(f32[2,128]{1,0:T(2,128)S(1)} %get-tuple-element.285), channel_id=1, replica_groups=mesh['member'=2,'section'=4,'atoms'=4] {'member'}, use_global_device_ids=true, to_apply=%region_10.11 | all-reduce | flops 256 | bytes 2048 | tf_op jit(solution)/shard_map/psum | solution.py:109
  190.8 0.7 fusion.80
  191.5 8.9 %pmax.7 = f32[2]{0:T(128)} all-reduce(f32[2]{0:T(128)S(1)} %get-tuple-element.283), channel_id=1, replica_groups=mesh['member'=2,'section'=4,'atoms'=4] {'atoms'}, use_global_device_ids=true, to_apply=%region_12.13 | all-reduce | flops 2 | bytes 16 | tf_op jit(solution)/shard_map/pmax | solution.py:111
  (81 shorter events, 6.2 us)
Async XLA Ops:
  0.6 47.2 %copy-start = (bf16[1,128,128]{2,1,0:T(8,128)(2,1)S(1)}, bf16[1,128,128]{2,1,0:T(8,128)(2,1)}, u32[]{:S(2)}) copy-start(bf16[1,128,128]{2,1,0:T(8,128)(2,1)} %param.15) | copy-start | bytes 98308
where the time goes:
time: 201 us; the launch traced here: 200 us
  blocking collectives  159 us (79%)
  matrix products  20.5 us (10%)
  other arithmetic  16.4 us (8%)
  local copies, waits for them, and re-layouts  3.21 us (2%)
    all_gather x8, blocking collectives, block_dev(): lax.all_gather(normed, 'atoms', axis=0, tiled=True)  98.7 us
    all_gather x1, blocking collectives, shards(): pos_all = lax.all_gather(positions, 'atoms', axis=2, tiled=True)  12.2 us
    reduce_sum x2, other arithmetic, geometry(): counts = jnp.sum(hit * mask.astype(jnp.float32)[:, :, None], 1)  11.9 us
    all_gather x1, blocking collectives, shards(): lax.all_gather(norm_gain, 'section', axis=1, tiled=True)  9.53 us
    all_gather x1, blocking collectives, shards(): lax.all_gather(proj_weight, 'section', axis=1, tiled=True)  9.27 us
    pmax x1, blocking collectives, shards(): max_dev = lax.pmax(jnp.max(atom_dev, -1), 'atoms')  8.87 us
    all_gather x1, blocking collectives, shards(): lax.all_gather(force_coef, 'section', axis=1, tiled=True)  7.81 us
    all_gather x1, blocking collectives, shards(): lax.all_gather(out_weight, 'section', axis=1, tiled=True)  7.68 us

commit v1 on v0

v1 whole, which is shorter than its diff:
```python
import math

import jax
import jax.numpy as jnp
from jax import lax
from jax.experimental import pallas as pl
from jax.experimental.pallas import tpu as pltpu
from jax.sharding import PartitionSpec as P

F32 = jnp.float32
BF16 = jnp.bfloat16
EXTRA = 8
NIBBLES = 8
WROWS = 16


def dest(axis_size, index, r):
    if axis_size & (axis_size - 1) == 0:
        return index ^ r
    return (index + r) % axis_size


def source(axis_size, index, r):
    if axis_size & (axis_size - 1) == 0:
        return index ^ r
    return (index - r) % axis_size


def back(axis_size, index, g):
    if axis_size & (axis_size - 1) == 0:
        return index ^ g
    return (index - g) % axis_size


def exchange(x, axis, axis_size, r):
    if r == 0:
        return x
    return lax.ppermute(x, axis, [(i, dest(axis_size, i, r)) for i in range(axis_size)])


def pack_kernel(n_section, n_atoms, pos_ref, typ_ref, nbr_ref, mask_ref, *refs):
    frames = pos_ref.shape[0]
    per_section = frames // n_section
    outs, (nbr_v, mask_v, sems) = refs[:per_section], refs[per_section:]
    first = lax.axis_index("section") * per_section
    mine = lax.axis_index("atoms") % per_section
    copies = []
    for x in range(per_section):
        frame = first + dest(per_section, mine, x)
        a = pltpu.make_async_copy(nbr_ref.at[frame], nbr_v.at[x], sems.at[x, 0])
        b = pltpu.make_async_copy(mask_ref.at[frame], mask_v.at[x], sems.at[x, 1])
        a.start()
        b.start()
        copies.append((frame, a, b))
    for x, (frame, a, b) in enumerate(copies):
        a.wait()
        b.wait()
        slots = nbr_v.shape[2]
        count = nbr_v.shape[1]
        eff = jnp.where(mask_v[x] != 0, nbr_v[x], -1).astype(F32)
        outs[x][:slots, :] = jnp.transpose(eff)
        pos = pos_ref[frame]
        typ = typ_ref[pl.ds(frame, 1), :].astype(F32)
        outs[x][slots:, :] = jnp.concatenate(
            [pos, typ, jnp.zeros((EXTRA - 4, count), F32)], axis=0
        )


def histogram(list_ref, slice_id, slots, total):
    low = total // NIBBLES
    count = list_ref.shape[2]
    iota = lax.broadcasted_iota(jnp.int32, (low, count), 0)

    def chunk(c, acc):
        even, odd = acc
        eff = list_ref[slice_id, pl.ds(c * 8, 8), :]
        hi = jnp.floor((eff + 0.5) * (1.0 / low))
        lo = jnp.where(eff < 0, -1.0, eff - hi * low).astype(jnp.int32)
        weight = jnp.left_shift(1, 4 * jnp.maximum(hi, 0.0).astype(jnp.int32))
        nib = jnp.zeros((low, count), jnp.int32)
        for s in range(8):
            nib = nib + jnp.where(iota == lo[s : s + 1, :], weight[s : s + 1, :], 0)
        even = even + (nib & 0x0F0F0F0F)
        odd = odd + (lax.shift_right_logical(nib, 4) & 0x0F0F0F0F)
        return even, odd

    zero = jnp.zeros((low, count), jnp.int32)
    even, odd = lax.fori_loop(0, slots // 8, chunk, (zero, zero))
    rows = []
    for n in range(NIBBLES):
        acc = odd if n % 2 else even
        rows.append((lax.shift_right_logical(acc, 8 * (n // 2)) & 0xFF).astype(F32))
    return rows


def dot(a, b):
    return lax.dot_general(a, b, (((1,), (0,)), ((), ())), preferred_element_type=F32)


def dot_t(a, b):
    return lax.dot_general(a, b, (((0,), (0,)), ((), ())), preferred_element_type=F32)


def main_kernel(n_section, n_atoms, heads, *refs):
    lists_in = refs[:n_atoms]
    weights_in = refs[n_atoms : n_atoms + n_section]
    table_ref, out_ref, list_v, w_v, p_v, h_v, f_v = refs[n_atoms + n_section :]
    slots = list_v.shape[1] - EXTRA
    count = list_v.shape[2]
    total = n_atoms * count
    width = table_ref.shape[1]
    head_dim = width // heads
    low = total // NIBBLES
    a_idx = lax.axis_index("atoms")
    s_idx = lax.axis_index("section")
    for r in range(n_atoms):
        list_v[source(n_atoms, a_idx, r)] = lists_in[r][...]
    for r in range(n_section):
        w_v[source(n_section, s_idx, r)] = weights_in[r][...]

    extra = jnp.concatenate([list_v[b, slots:, :] for b in range(n_atoms)], axis=1)
    pos_col = jnp.transpose(extra)
    for b in range(n_atoms):
        rows = histogram(list_v, b, slots, total)
        for n in range(NIBBLES):
            part = pos_col[n * low : (n + 1) * low]
            dist = None
            for c in range(3):
                delta = part[:, c : c + 1] - extra[c : c + 1, b * count : (b + 1) * count]
                dist = delta * delta if dist is None else dist + delta * delta
            p_v[n * low : (n + 1) * low, b * count : (b + 1) * count] = (
                0.5 * rows[n] / (1.0 + 0.125 * dist)
            )

    types = extra[3:4, :].astype(jnp.int32)
    onehot = (lax.broadcasted_iota(jnp.int32, (table_ref.shape[0], total), 0) == types).astype(BF16)
    h_v[...] = dot_t(table_ref[...], onehot).astype(BF16).astype(F32)
    pos = extra[:3, :]
    pos_hi = pos.astype(BF16).astype(F32)
    pos_lo = pos - pos_hi
    tail = jnp.concatenate(
        [pos_hi, pos_lo, jnp.ones((1, total), F32), jnp.zeros((9, total), F32)], axis=0
    ).astype(BF16)
    f_v[...] = jnp.zeros_like(f_v)
    scale = 0.5 / math.sqrt(head_dim)
    tile = min(256, total)

    def block(b, carry):
        w = w_v[b]
        gain = jnp.transpose(
            jnp.broadcast_to(w[width : width + 1, :width].astype(F32), (width, width))
        )[:, :1]
        coef = w[width : width + 1, width : width + heads].astype(F32)
        h = h_v[...]
        norm = lax.rsqrt(jnp.mean(h * h, axis=0, keepdims=True) + 1e-06)
        x = (h * norm * gain).astype(BF16)
        wmat = w[:width]
        qkv = dot_t(wmat[:, : 3 * width], x)
        q = (qkv[:width] * scale).astype(BF16)
        k = jnp.transpose(qkv[width : 2 * width]).astype(BF16)
        v = qkv[2 * width :].astype(BF16)
        msgs = []
        for t in range(total // tile):
            lanes = slice(t * tile, (t + 1) * tile)
            p = p_v[:, lanes]
            parts = []
            force = None
            for hd in range(heads):
                rows = slice(hd * head_dim, (hd + 1) * head_dim)
                pieces = []
                if hd > 0:
                    pieces.append(jnp.zeros((hd * head_dim, tile), BF16))
                pieces.append(q[rows, lanes])
                if hd < heads - 1:
                    pieces.append(jnp.zeros(((heads - 1 - hd) * head_dim, tile), BF16))
                score = dot(k, jnp.concatenate(pieces, axis=0))
                g = (p * jnp.tanh(score) + p).astype(BF16)
                lhs = jnp.concatenate([v[rows], tail], axis=0)
                res = dot(lhs, g)
                parts.append(res[:head_dim])
                term = coef[:, hd : hd + 1] * res[head_dim : head_dim + 8]
                force = term if force is None else force + term
            f_v[:, lanes] = f_v[:, lanes] + force
            msgs.append(jnp.concatenate(parts, axis=0))
        msg = (jnp.concatenate(msgs, axis=1) / slots).astype(BF16)
        h_v[...] = (h + dot_t(wmat[:, 3 * width :], msg)).astype(BF16).astype(F32)
        return carry

    lax.fori_loop(0, n_section, block, 0)
    f = f_v[...]
    force = (f[0:3] + f[3:6] - pos * f[6:7]) / slots
    out_ref[...] = jnp.concatenate([force, jnp.zeros((5, total), F32)], axis=0)


def shards(n_member, n_section, n_atoms):
    def body(
        positions,
        atom_types,
        neighbors,
        nbr_mask,
        type_table,
        norm_gain,
        proj_weight,
        out_weight,
        force_coef,
    ):
        frames = positions.shape[0]
        per_section = frames // n_section
        count, slots = neighbors.shape[1:]
        total = count * n_atoms
        heads = force_coef.shape[-1]
        width = out_weight.shape[-1]
        any_spec = pl.BlockSpec(memory_space=pl.ANY)
        vmem = pl.BlockSpec(memory_space=pltpu.VMEM)

        own_w = jnp.concatenate([proj_weight[0, 0], out_weight[0, 0]], axis=1)
        row = jnp.concatenate(
            [norm_gain[0, 0], force_coef[0, 0], jnp.zeros((3 * width - heads,), BF16)]
        )
        own_w = jnp.concatenate(
            [own_w, jnp.broadcast_to(row[None], (WROWS, 4 * width))], axis=0
        )
        weights = [exchange(own_w, "section", n_section, r) for r in range(n_section)]

        packed = pl.pallas_call(
            lambda *refs: pack_kernel(n_section, n_atoms, *refs),
            out_shape=[jax.ShapeDtypeStruct((slots + EXTRA, count), F32)] * per_section,
            in_specs=[vmem, vmem, any_spec, any_spec],
            out_specs=[vmem] * per_section,
            scratch_shapes=[
                pltpu.VMEM((per_section, count, slots), jnp.int32),
                pltpu.VMEM((per_section, count, slots), jnp.int32),
                pltpu.SemaphoreType.DMA((per_section, 2)),
            ],
            name="pack",
        )(positions, atom_types, neighbors, nbr_mask)
        lists = [
            exchange(packed[r % per_section], "atoms", n_atoms, r) for r in range(n_atoms)
        ]

        force = pl.pallas_call(
            lambda *refs: main_kernel(n_section, n_atoms, heads, *refs),
            out_shape=jax.ShapeDtypeStruct((8, total), F32),
            in_specs=[vmem] * (n_atoms + n_section + 1),
            out_specs=vmem,
            scratch_shapes=[
                pltpu.VMEM((n_atoms, slots + EXTRA, count), F32),
                pltpu.VMEM((n_section, width + WROWS, 4 * width), BF16),
                pltpu.VMEM((total, total), F32),
                pltpu.VMEM((width, total), F32),
                pltpu.VMEM((8, total), F32),
            ],
            name="frame",
        )(*lists, *weights, type_table[0])

        others = [force[:3]] + [
            exchange(force, "member", n_member, r)[:3] for r in range(1, n_member)
        ]
        mean = sum(others) / n_member
        spread = sum(jnp.sum((f - mean) * (f - mean), 0, keepdims=True) for f in others)
        dev = jnp.sqrt(spread / n_member)
        result = jnp.concatenate([mean, dev, jnp.zeros((4, total), F32)], axis=0)
        mine = lax.axis_index("atoms") % per_section
        got = jnp.stack(
            [result] + [exchange(result, "atoms", n_atoms, r) for r in range(1, per_section)]
        )
        got = jnp.stack(
            [
                lax.dynamic_index_in_dim(got, back(per_section, mine, g), 0, keepdims=False)
                for g in range(per_section)
            ]
        )
        own = lax.dynamic_slice_in_dim(got, lax.axis_index("atoms") * count, count, 2)
        return own[:, 3], jnp.max(got[:, 3], -1), own[:, :3]

    return body


def solution(mesh):
    sizes = mesh.shape
    return jax.shard_map(
        shards(sizes["member"], sizes["section"], sizes["atoms"]),
        mesh=mesh,
        in_specs=(
            P(None, None, "atoms"),
            P(None, "atoms"),
            P(None, "atoms", None),
            P(None, "atoms", None),
            P("member", None, None),
            P("member", "section", None),
            P("member", "section", None, None),
            P("member", "section", None, None),
            P("member", "section", None),
        ),
        out_specs=(P("section", "atoms"), P("section"), P("section", None, "atoms")),
        check_vma=False,
    )
```

time: 201 us -> 47.9 us (0.24)
  blocking collectives: 159 us -> 0 us
  matrix products: 20.5 us -> 0 us
  Pallas kernels: 0 us -> 20.2 us
  starting transfers between devices: 0 us -> 14.3 us
  other arithmetic: 16.4 us -> 2.47 us
  waiting for transfers between devices: 0 us -> 6.6 us
    all_gather x13 -> x0, blocking collectives: 145 us -> none  [the longest x8 98.7 us: block_dev(): lax.all_gather(normed, 'atoms', axis=0, tiled=True)]
    dot_general x54 -> x0, matrix products: 20.5 us -> none  [the longest x8 5.1 us: block_dev(): force = jnp.einsum('aj,caj->ca', pair_coef, delta) / slots]
    pallas_call x0 -> x2, Pallas kernels: none -> 20.2 us  [the longest x1 17.7 us: body(): pl.pallas_call(lambda *refs: main_kernel(n_section, n_atoms, heads, *refs...]
    ppermute x0 -> x8, starting transfers between devices: none -> 14.3 us  [exchange(): lax.ppermute(x, axis, [(i, dest(axis_size, i, r)) for i in range(axis_siz...]
    reduce_sum x5 -> x1, other arithmetic: 12.8 us -> 0.74 us  [body(): jnp.sum((f - mean) * (f - mean), 0, keepdims=True)]
    pmax x1 -> x0, blocking collectives: 8.87 us -> none  [shards(): max_dev = lax.pmax(jnp.max(atom_dev, -1), 'atoms')]
    ppermute x0 -> x8, waiting for transfers between devices: none -> 6.6 us  [exchange(): lax.ppermute(x, axis, [(i, dest(axis_size, i, r)) for i in range(axis_siz...]
    psum x2 -> x0, blocking collectives: 4.92 us -> none  [the longest x1 2.47 us: shards(): mean_force = lax.psum(own, 'member') / members]
  transfers between devices with their start and end apart: 0 -> 8, of which waited for: 0 -> 4; matrix products, arithmetic and copies ran while one was open for 0% -> 1% of each run, Pallas kernels for 0% -> 5%
where the time goes in v1:
time: 47.9 us; the launch traced here: 47.5 us
  Pallas kernels  20.2 us (42%)
  starting transfers between devices  14.3 us (30%)
  waiting for transfers between devices  6.6 us (14%)
  local copies, waits for them, and re-layouts  3.23 us (7%)
  other arithmetic  2.47 us (5%)
  between operations  0.75 us (2%)
    pallas_call x1, Pallas kernels, body(): pl.pallas_call(lambda *refs: main_kernel(n_section, n_atoms, heads, *refs...  17.7 us
    ppermute x8, starting transfers between devices, exchange(): lax.ppermute(x, axis, [(i, dest(axis_size, i, r)) for i in range(axis_siz...  14.3 us
    ppermute x8, waiting for transfers between devices, exchange(): lax.ppermute(x, axis, [(i, dest(axis_size, i, r)) for i in range(axis_siz...  6.6 us
    unnamed x22, local copies, waits for them, and re-layouts  2.57 us
    pallas_call x1, Pallas kernels, body(): pl.pallas_call(lambda *refs: pack_kernel(n_section, n_atoms, *refs), out_...  2.45 us
  transfers between devices with their start and end apart: 8, of which 4 were waited for; matrix products, arithmetic and copies ran while one was open for 1% of the time, Pallas kernels for 5%

profile of v1, /device:TPU:0, one launch (start us, length us, event | category | flops | bytes accessed | tf_op | source)
XLA Modules:
  0.0 47.5 jit_solution(10160317322800651132)
XLA Ops:
  0.6 0.0 copy-start.8
  0.6 0.0 copy-start.9
  0.7 0.6 %copy-done.8 = bf16[1,1,4]{2,1,0:T(2,128)(2,1)S(1)} copy-done((bf16[1,1,4]{2,1,0:T(2,128)(2,1)S(1)}, bf16[1,1,4]{2,1,0:T(2,128)(2,1)}, u32[]{:S(2)}) %copy-start.8) | copy-done | bytes 32
  1.3 0.0 copy-done.9
  1.3 0.1 pad_maximum_fusion.2
  1.4 0.0 copy-start.7
  1.4 0.9 %pad_maximum_fusion.refs_4_ = bf16[144,512]{1,0:T(8,128)(2,1)S(1)} fusion(bf16[16,512]{1,0:T(8,128)(2,1)S(1)} %broadcast_in_dim.7, bf16[128,128]{1,0:T(8,128)(2,1)} %bitcast.11, bf16[128,384]{1,0:T(8,128)(2,1)} %bitcast.10), kind=kLoop, calls=%fused_computation | loop fusion | flops 442368 | bytes 294912 | tf_op jit(solution)/shard_map/concatenate | solution.py:220
  2.3 0.0 copy-start
  2.3 3.0 %collective-permute-start.3 = (bf16[144,512]{1,0:T(8,128)(2,1)S(1)}, bf16[144,512]{1,0:T(8,128)(2,1)S(1)}, u32[]{:S(2)}, u32[]{:S(2)}) collective-permute-start(bf16[144,512]{1,0:T(8,128)(2,1)S(1)} %pad_maximum_fusion.refs_4_), channel_id=1, source_target_pairs={{0,4},{4,0},{8,12},{12,8},{1,5},{5,1},{9,13},{13,9},{2,6},{6,2},{1... | collective-permute-start | bytes 442376 | tf_op jit(solution)/shard_map/ppermute | solution.py:38
  5.4 1.5 %collective-permute-start.4 = (bf16[144,512]{1,0:T(8,128)(2,1)S(1)}, bf16[144,512]{1,0:T(8,128)(2,1)S(1)}, u32[]{:S(2)}, u32[]{:S(2)}) collective-permute-start(bf16[144,512]{1,0:T(8,128)(2,1)S(1)} %pad_maximum_fusion.refs_4_), channel_id=1, source_target_pairs={{0,8},{4,12},{8,0},{12,4},{1,9},{5,13},{9,1},{13,5},{2,10},{6,14},... | collective-permute-start | bytes 442376 | tf_op jit(solution)/shard_map/ppermute | solution.py:38
  6.9 0.0 collective-permute-start.5
  6.9 0.0 copy-done.7
  6.9 0.6 %copy.14.refs_0_ = f32[8,3,128]{2,1,0:T(4,128)} copy(f32[8,3,128]{2,0,1:T(8,128)S(1)} %copy-done.7) | data formatting | bytes 24576 | tf_op args[0]
  7.5 2.5 %pack.1 = (f32[136,128]{1,0:T(8,128)}, f32[136,128]{1,0:T(8,128)}) custom-call(f32[8,3,128]{2,1,0:T(4,128)} %copy.14.refs_0_, s32[8,128]{1,0:T(8,128)} %refs_1_.1, s32[8,128,128]{2,1,0:T(8,128)} %refs_2_.1, s32[8,128,128]{2,1,0:T(8,128)} %refs_3_.1), custom_call_target="tpu_custom_call" | custom-call | tf_op jit(solution)/shard_map/pack/pallas_call | solution.py:225
  10.0 0.0 copy-done
  10.0 2.1 %collective-permute-start = (f32[136,128]{1,0:T(8,128)}, f32[136,128]{1,0:T(8,128)S(1)}, u32[]{:S(2)}, u32[]{:S(2)}) collective-permute-start(f32[136,128]{1,0:T(8,128)} %get-tuple-element.6), channel_id=1, source_target_pairs={{0,1},{1,0},{2,3},{3,2},{4,5},{5,4},{6,7},{7,6},{8,9},{9,8},{10,11... | collective-permute-start | bytes 208904 | tf_op jit(solution)/shard_map/ppermute | solution.py:38
  12.1 2.6 %collective-permute-start.1 = (f32[136,128]{1,0:T(8,128)}, f32[136,128]{1,0:T(8,128)S(1)}, u32[]{:S(2)}, u32[]{:S(2)}) collective-permute-start(f32[136,128]{1,0:T(8,128)} %get-tuple-element.5.refs_0_), channel_id=1, source_target_pairs={{0,2},{1,3},{2,0},{3,1},{4,6},{5,7},{6,4},{7,5},{8,10},{9,11},{10,... | collective-permute-start | bytes 208904 | tf_op jit(solution)/shard_map/ppermute | solution.py:38
  14.7 0.0 collective-permute-done.refs_1_
  14.7 0.0 copy-start.4
  14.7 4.0 %collective-permute-start.2 = (f32[136,128]{1,0:T(8,128)}, f32[136,128]{1,0:T(8,128)S(1)}, u32[]{:S(2)}, u32[]{:S(2)}) collective-permute-start(f32[136,128]{1,0:T(8,128)} %get-tuple-element.6), channel_id=1, source_target_pairs={{0,3},{1,2},{2,1},{3,0},{4,7},{5,6},{6,5},{7,4},{8,11},{9,10},{10,... | collective-permute-start | bytes 208904 | tf_op jit(solution)/shard_map/ppermute | solution.py:38
  18.6 0.9 %collective-permute-done.1.refs_2_ = f32[136,128]{1,0:T(8,128)S(1)} collective-permute-done((f32[136,128]{1,0:T(8,128)}, f32[136,128]{1,0:T(8,128)S(1)}, u32[]{:S(2)}, u32[]{:S(2)}) %collective-permute-start.1) | collective-permute-done | bytes 69664 | tf_op jit(solution)/shard_map/ppermute | solution.py:38
  19.5 0.0 copy-start.5
  19.5 1.7 %collective-permute-done.2.refs_3_ = f32[136,128]{1,0:T(8,128)S(1)} collective-permute-done((f32[136,128]{1,0:T(8,128)}, f32[136,128]{1,0:T(8,128)S(1)}, u32[]{:S(2)}, u32[]{:S(2)}) %collective-permute-start.2) | collective-permute-done | bytes 69664 | tf_op jit(solution)/shard_map/ppermute | solution.py:38
  21.2 0.0 copy-start.6
  21.2 0.0 collective-permute-done.3.refs_5_
  21.3 0.0 copy-start.1
  21.3 0.0 collective-permute-done.4.refs_6_
  21.3 0.0 copy-start.2
  21.3 0.0 collective-permute-done.5.refs_7_
  21.3 0.0 copy-start.3
  21.3 0.0 copy-done.4
  21.3 0.0 copy-done.5
  21.3 0.6 %copy-done.6 = f32[136,128]{1,0:T(8,128)} copy-done((f32[136,128]{1,0:T(8,128)}, f32[136,128]{1,0:T(8,128)S(1)}, u32[]{:S(2)}) %copy-start.6) | copy-done | bytes 69656
  21.9 0.1 copy-done.1
  21.9 0.1 copy-done.2
  22.0 0.0 copy-done.3
  22.0 17.7 %frame.1 = f32[8,512]{1,0:T(8,128)} custom-call(f32[136,128]{1,0:T(8,128)} %get-tuple-element.5.refs_0_, f32[136,128]{1,0:T(8,128)} %copy-done.4, f32[136,128]{1,0:T(8,128)} %copy-done.5, f32[136,128]{1,0:T(8,128)} %copy-done.6, bf16[144,512]{1,0:T(8,128)(2,1)} %copy-done, bf16[144,512]{1,0:T(8,128)(2,1)} %copy-done.1, bf16[144,512]{1,0:T(8,128)(2,1)} %copy-done.2, ...), custom_call_target="tpu_custom_call" | custom-call | tf_op jit(solution)/shard_map/frame/pallas_call | solution.py:241
  39.7 0.0 collective-permute-start.6
  39.8 0.1 pad.6.clone
  39.8 1.3 %collective-permute-done.6 = f32[8,512]{1,0:T(8,128)S(1)} collective-permute-done((f32[8,512]{1,0:T(8,128)}, f32[8,512]{1,0:T(8,128)S(1)}, u32[]{:S(2)}, u32[]{:S(2)}) %collective-permute-start.6) | collective-permute-done | bytes 16416 | tf_op jit(solution)/shard_map/ppermute | solution.py:38
  41.1 0.7 %multiply_reduce_fusion = (f32[512]{0:T(512)S(1)}, f32[512]{0:T(512)S(1)}, f32[3,512]{1,0:T(4,128)S(1)}) fusion(f32[8,512]{1,0:T(8,128)S(1)} %collective-permute-done.6, f32[8,512]{1,0:T(8,128)} %frame.1), kind=kLoop, calls=%fused_computation.11 | loop fusion | flops 11264 | bytes 22528 | tf_op jit(solution)/shard_map/reduce_sum | solution.py:260
  41.9 0.1 maximum_maximum_fusion
  42.0 1.1 %collective-permute-start.7 = (f32[8,512]{1,0:T(8,128)S(1)}, f32[8,512]{1,0:T(8,128)S(1)}, u32[]{:S(2)}, u32[]{:S(2)}) collective-permute-start(f32[8,512]{1,0:T(8,128)S(1)} %get-tuple-element.15), channel_id=1, source_target_pairs={{0,1},{1,0},{2,3},{3,2},{4,5},{5,4},{6,7},{7,6},{8,9},{9,8},{10,11... | collective-permute-start | bytes 49160 | tf_op jit(solution)/shard_map/ppermute | solution.py:38
  43.0 2.7 %collective-permute-done.7 = f32[8,512]{1,0:T(8,128)S(1)} collective-permute-done((f32[8,512]{1,0:T(8,128)S(1)}, f32[8,512]{1,0:T(8,128)S(1)}, u32[]{:S(2)}, u32[]{:S(2)}) %collective-permute-start.7) | collective-permute-done | bytes 16416 | tf_op jit(solution)/shard_map/ppermute | solution.py:38
  45.7 0.6 %fusion.3 = f32[2]{0:T(128)} fusion(f32[1,8,512]{2,1,0:T(8,128)S(1)} %get-tuple-element.13, f32[1,8,512]{2,1,0:T(8,128)S(1)} %get-tuple-element.14), kind=kLoop, calls=%fused_computation.15 | loop fusion | flops 2046 | bytes 32776 | tf_op jit(solution)/shard_map/reduce_max | solution.py:274
  46.4 0.6 %slice.22 = f32[2,1,128]{2,1,0:T(1,128)} slice(f32[2,8,128]{2,1,0:T(8,128)S(1)} %fusion.2), slice={[0:2], [3:4], [0:128]} | slice | bytes 2048 | tf_op jit(solution)/shard_map/slice | solution.py:274
  46.9 0.6 %copy.15 = f32[2,3,128]{2,0,1:T(2,128)} copy(f32[2,3,128]{2,1,0:T(4,128)S(1)} %slice.23) | data formatting | bytes 6144
  (7 shorter events, 0.0 us)
Async XLA Ops:
  0.6 0.7 %copy-start.8 = (bf16[1,1,4]{2,1,0:T(2,128)(2,1)S(1)}, bf16[1,1,4]{2,1,0:T(2,128)(2,1)}, u32[]{:S(2)}) copy-start(bf16[1,1,4]{2,1,0:T(2,128)(2,1)} %param.17) | copy-start | bytes 28
  0.6 0.7 %copy-start.9 = (bf16[1,1,128]{2,1,0:T(2,128)(2,1)S(1)}, bf16[1,1,128]{2,1,0:T(2,128)(2,1)}, u32[]{:S(2)}) copy-start(bf16[1,1,128]{2,1,0:T(2,128)(2,1)} %param.14) | copy-start | bytes 772
  1.4 5.5 %copy-start.7 = (f32[8,3,128]{2,0,1:T(8,128)S(1)}, f32[8,3,128]{2,0,1:T(8,128)}, u32[]{:S(2)}) copy-start(f32[8,3,128]{2,0,1:T(8,128)} %param.9) | copy-start | bytes 36868
  2.3 7.7 %copy-start = (bf16[144,512]{1,0:T(8,128)(2,1)}, bf16[144,512]{1,0:T(8,128)(2,1)S(1)}, u32[]{:S(2)}) copy-start(bf16[144,512]{1,0:T(8,128)(2,1)S(1)} %pad_maximum_fusion.refs_4_) | copy-start | bytes 442372
  2.3 18.9 %collective-permute-start.3 = (bf16[144,512]{1,0:T(8,128)(2,1)S(1)}, bf16[144,512]{1,0:T(8,128)(2,1)S(1)}, u32[]{:S(2)}, u32[]{:S(2)}) collective-permute-start(bf16[144,512]{1,0:T(8,128)(2,1)S(1)} %pad_maximum_fusion.refs_4_), channel_id=1, source_target_pairs={{0,4},{4,0},{8,12},{12,8},{1,5},{5,1},{9,13},{13,9},{2,6},{6,2},{1... | collective-permute-start | bytes 442376 | tf_op jit(solution)/shard_map/ppermute | solution.py:38
  5.4 15.9 %collective-permute-start.4 = (bf16[144,512]{1,0:T(8,128)(2,1)S(1)}, bf16[144,512]{1,0:T(8,128)(2,1)S(1)}, u32[]{:S(2)}, u32[]{:S(2)}) collective-permute-start(bf16[144,512]{1,0:T(8,128)(2,1)S(1)} %pad_maximum_fusion.refs_4_), channel_id=1, source_target_pairs={{0,8},{4,12},{8,0},{12,4},{1,9},{5,13},{9,1},{13,5},{2,10},{6,14},... | collective-permute-start | bytes 442376 | tf_op jit(solution)/shard_map/ppermute | solution.py:38
  6.9 14.4 %collective-permute-start.5 = (bf16[144,512]{1,0:T(8,128)(2,1)S(1)}, bf16[144,512]{1,0:T(8,128)(2,1)S(1)}, u32[]{:S(2)}, u32[]{:S(2)}) collective-permute-start(bf16[144,512]{1,0:T(8,128)(2,1)S(1)} %pad_maximum_fusion.refs_4_), channel_id=1, source_target_pairs={{0,12},{4,8},{8,4},{12,0},{1,13},{5,9},{9,5},{13,1},{2,14},{6,10},... | collective-permute-start | bytes 442376 | tf_op jit(solution)/shard_map/ppermute | solution.py:38
  10.0 4.7 %collective-permute-start = (f32[136,128]{1,0:T(8,128)}, f32[136,128]{1,0:T(8,128)S(1)}, u32[]{:S(2)}, u32[]{:S(2)}) collective-permute-start(f32[136,128]{1,0:T(8,128)} %get-tuple-element.6), channel_id=1, source_target_pairs={{0,1},{1,0},{2,3},{3,2},{4,5},{5,4},{6,7},{7,6},{8,9},{9,8},{10,11... | collective-permute-start | bytes 208904 | tf_op jit(solution)/shard_map/ppermute | solution.py:38
  12.1 7.4 %collective-permute-start.1 = (f32[136,128]{1,0:T(8,128)}, f32[136,128]{1,0:T(8,128)S(1)}, u32[]{:S(2)}, u32[]{:S(2)}) collective-permute-start(f32[136,128]{1,0:T(8,128)} %get-tuple-element.5.refs_0_), channel_id=1, source_target_pairs={{0,2},{1,3},{2,0},{3,1},{4,6},{5,7},{6,4},{7,5},{8,10},{9,11},{10,... | collective-permute-start | bytes 208904 | tf_op jit(solution)/shard_map/ppermute | solution.py:38
  14.7 6.6 %copy-start.4 = (f32[136,128]{1,0:T(8,128)}, f32[136,128]{1,0:T(8,128)S(1)}, u32[]{:S(2)}) copy-start(f32[136,128]{1,0:T(8,128)S(1)} %collective-permute-done.refs_1_) | copy-start | bytes 208900
  14.7 6.6 %collective-permute-start.2 = (f32[136,128]{1,0:T(8,128)}, f32[136,128]{1,0:T(8,128)S(1)}, u32[]{:S(2)}, u32[]{:S(2)}) collective-permute-start(f32[136,128]{1,0:T(8,128)} %get-tuple-element.6), channel_id=1, source_target_pairs={{0,3},{1,2},{2,1},{3,0},{4,7},{5,6},{6,5},{7,4},{8,11},{9,10},{10,... | collective-permute-start | bytes 208904 | tf_op jit(solution)/shard_map/ppermute | solution.py:38
  19.5 1.8 %copy-start.5 = (f32[136,128]{1,0:T(8,128)}, f32[136,128]{1,0:T(8,128)S(1)}, u32[]{:S(2)}) copy-start(f32[136,128]{1,0:T(8,128)S(1)} %collective-permute-done.1.refs_2_) | copy-start | bytes 208900
  21.2 0.6 %copy-start.6 = (f32[136,128]{1,0:T(8,128)}, f32[136,128]{1,0:T(8,128)S(1)}, u32[]{:S(2)}) copy-start(f32[136,128]{1,0:T(8,128)S(1)} %collective-permute-done.2.refs_3_) | copy-start | bytes 208900
  21.3 0.7 %copy-start.1 = (bf16[144,512]{1,0:T(8,128)(2,1)}, bf16[144,512]{1,0:T(8,128)(2,1)S(1)}, u32[]{:S(2)}) copy-start(bf16[144,512]{1,0:T(8,128)(2,1)S(1)} %collective-permute-done.3.refs_5_) | copy-start | bytes 442372
  21.3 0.7 %copy-start.2 = (bf16[144,512]{1,0:T(8,128)(2,1)}, bf16[144,512]{1,0:T(8,128)(2,1)S(1)}, u32[]{:S(2)}) copy-start(bf16[144,512]{1,0:T(8,128)(2,1)S(1)} %collective-permute-done.4.refs_6_) | copy-start | bytes 442372
  21.3 0.7 %copy-start.3 = (bf16[144,512]{1,0:T(8,128)(2,1)}, bf16[144,512]{1,0:T(8,128)(2,1)S(1)}, u32[]{:S(2)}) copy-start(bf16[144,512]{1,0:T(8,128)(2,1)S(1)} %collective-permute-done.5.refs_7_) | copy-start | bytes 442372
  39.7 1.4 %collective-permute-start.6 = (f32[8,512]{1,0:T(8,128)}, f32[8,512]{1,0:T(8,128)S(1)}, u32[]{:S(2)}, u32[]{:S(2)}) collective-permute-start(f32[8,512]{1,0:T(8,128)} %frame.1), channel_id=1, source_target_pairs={{0,16},{16,0},{1,17},{17,1},{2,18},{18,2},{3,19},{19,3},{4,20},{20... | collective-permute-start | bytes 49160 | tf_op jit(solution)/shard_map/ppermute | solution.py:38
  42.0 3.7 %collective-permute-start.7 = (f32[8,512]{1,0:T(8,128)S(1)}, f32[8,512]{1,0:T(8,128)S(1)}, u32[]{:S(2)}, u32[]{:S(2)}) collective-permute-start(f32[8,512]{1,0:T(8,128)S(1)} %get-tuple-element.15), channel_id=1, source_target_pairs={{0,1},{1,0},{2,3},{3,2},{4,5},{5,4},{6,7},{7,6},{8,9},{9,8},{10,11... | collective-permute-start | bytes 49160 | tf_op jit(solution)/shard_map/ppermute | solution.py:38
